TPU v7x, 32 devices: a whole 2x2x4 slice. The times are simulated.
32 devices in a mesh: grp: 2 (over y), mode: 8 (over z, x), node: 2 (over core).
Axes of the slice: x: 2, y: 2, z: 4, core: 2. Of those that a mesh axis runs over, the one named last changes fastest.
Arguments:
- mode_basis: float32 [4096, 4096], P('mode', 'node'), may hold values from -6 to 6
- mode_scales: float32 [4096], P('mode'), may hold values from 0.003 to 0.02
- mean_log: float32 [4096], P(('node', 'mode')), may hold values from -0.5 to 0.5
- sample_seeds: int32 [4096], P('grp'), parts along dimension 0, may hold values from 0 to 1073741823
Outputs:
- modulus: float32 [4096, 4096], P(('node', 'mode'), 'grp'), parts along dimension 1
- sample_means: float32 [4096], P('grp'), parts along dimension 0
There are 2 independent parts, one for each index of `grp`. A program takes and returns all parts, laid end to end along the dimension named above; an argument that names none is the same for every part. Nothing has to cross between parts.
All inputs are finite; a program needn't handle non-finite values.
Results may differ from a plain program's by a relative error of at most 0.00005.
Values sent between devices are 32-bit elements; how exact they have to be, the bound alone decides.
No kernel may reach another device: no remote copies, remote signals or barrier semaphores. Data moves between devices by JAX's collectives and lax.ppermute only.
A program may use at most 64 MiB of HBM per device.

v0:
```python
import math

import jax
import jax.numpy as jnp
from jax import lax
from jax.sharding import PartitionSpec as P


def scramble(seed_words, counter_words):
    mixed_word = seed_words * -1640531527 + counter_words * 668265261
    mixed_word = mixed_word ^ mixed_word >> 15 & 131071
    mixed_word = mixed_word * -2048144789
    mixed_word = mixed_word ^ mixed_word >> 13 & 524287
    mixed_word = mixed_word * -1028477387
    mixed_word = mixed_word ^ mixed_word >> 16 & 65535
    return mixed_word


def normals(sample_seeds, mode_start, mode_count):
    mode_ids = mode_start + jnp.arange(mode_count, dtype=jnp.int32)
    seed_words = sample_seeds[None, :]
    counter_words = (2 * mode_ids)[:, None]
    first_word = scramble(seed_words, counter_words)
    second_word = scramble(seed_words, counter_words + 1)
    first_unit = ((first_word & 16777215).astype(jnp.float32) + 0.5) * (1.0 / 16777216.0)
    second_unit = ((second_word & 16777215).astype(jnp.float32) + 0.5) * (1.0 / 16777216.0)
    radius = jnp.sqrt(-2.0 * jnp.log(first_unit))
    return radius * jnp.cos(2.0 * math.pi * second_unit)


def contract_all(all_modes, sample_seeds):
    mode_total = all_modes.shape[0]
    block_modes = min(512, mode_total)
    block_count = mode_total // block_modes
    start_total = jnp.zeros((all_modes.shape[1], sample_seeds.shape[0]), jnp.float32)

    def add_block(block, total):
        first_mode = (block * block_modes).astype(jnp.int32)
        rows = lax.dynamic_slice_in_dim(all_modes, first_mode, block_modes, 0)
        coeffs = normals(sample_seeds, first_mode, block_modes)
        return total + lax.dot_general(
            rows,
            coeffs,
            (((0,), (0,)), ((), ())),
            precision=lax.Precision.HIGHEST,
            preferred_element_type=jnp.float32,
        )

    return lax.fori_loop(0, block_count, add_block, start_total)


def on_device(mode_basis, mode_scales, mean_log, sample_seeds):
    own_rows = mean_log.shape[0]
    scaled = mode_scales[:, None] * mode_basis
    gathered = lax.all_to_all(scaled, "mode", split_axis=1, concat_axis=0, tiled=True)
    summed = contract_all(gathered, sample_seeds)
    modulus = jnp.exp(mean_log[:, None] + summed)
    totals = lax.psum(jnp.sum(modulus, axis=0), ("mode", "node"))
    node_count = own_rows * lax.axis_size("mode") * lax.axis_size("node")
    return (modulus, totals / node_count)


def solution(mesh):
    return jax.shard_map(
        on_device,
        mesh=mesh,
        in_specs=(P("mode", "node"), P("mode"), P(("node", "mode")), P("grp")),
        out_specs=(P(("node", "mode"), "grp"), P("grp")),
        check_vma=False,
    )
```

profile of v0, /device:TPU:0, one launch (start us, length us, event | category | flops | bytes accessed | tf_op | source)
XLA Modules:
  0.0 334.7 jit_solution(1991284625481277206)
XLA Ops:
  0.6 2.5 broadcast_multiply_fusion.1
  3.2 2.4 copy.9
  5.5 0.0 copy-start
  5.5 7.4 %all-to-all-start = ((f32[512,8,256]{2,0,1:T(8,128)}), f32[512,8,256]{2,0,1:T(8,128)}, u32[]{:S(2)}, u32[]{:S(2)}) async-start(f32[512,8,256]{2,0,1:T(8,128)} %bitcast.8), calls=%async_computation | async-start | bytes 8388608 | tf_op jit(solution)/shard_map/all_to_all | solution.py:55
  12.9 93.3 %all-to-all-done = f32[512,8,256]{2,0,1:T(8,128)} async-done(((f32[512,8,256]{2,0,1:T(8,128)}), f32[512,8,256]{2,0,1:T(8,128)}, u32[]{:S(2)}, u32[]{:S(2)}) %all-to-all-start) | async-done | bytes 4194336 | tf_op jit(solution)/shard_map/all_to_all | solution.py:55
  106.2 0.0 copy-done
  106.2 0.0 copy-start.1
  106.2 194.2 %while.16 = (s32[]{:T(128)}, f32[256,2048]{1,0:T(8,128)S(1)}, f32[4096,256]{1,0:T(8,128)}, s32[2048]{0:T(1024)S(1)}, s32[]{:T(128)}, /*index=5*/s32[]{:T(128)}, s32[]{:T(128)}, s32[]{:T(128)}) while((s32[]{:T(128)}, f32[256,2048]{1,0:T(8,128)S(1)}, f32[4096,256]{1,0:T(8,128)}, s32[2048]{0:T(1024)S(1)}, s32[]{:T(128)}, ...), condition=%wide.region_1.0_spmd.clone, body=%wide.region_0.0_spmd.clone.sunk | while | flops 3257930240 | bytes 4751509 | solution.py:49
  106.3 24.2 %fusion.75 = f32[256,2048]{1,0:T(8,128)S(1)} fusion(f32[256,2048]{1,0:T(8,128)S(1)} %get-tuple-element.179, s32[512]{0:T(512)S(1)} %get-tuple-element.168, s32[512]{0:T(512)S(1)} %get-tuple-element.169, s32[2048]{0:T(1024)S(1)} %broadcast_multiply_fusion.4, pred[]{:T(512)S(6)} %compare.3, f32[4096,256]{1,0:T(8,128)} %get-tuple-element.188, ...), kind=kOutput, calls=%fused_computation.36.clone.1 | convolution fusion | flops 3257925632 | bytes 4730885 | tf_op jit(solution)/shard_map/while/body/eval_jaxpr/dot_general | solution.py:41
  130.5 24.2 %fusion.75 = f32[256,2048]{1,0:T(8,128)S(1)} fusion(f32[256,2048]{1,0:T(8,128)S(1)} %get-tuple-element.179, s32[512]{0:T(512)S(1)} %get-tuple-element.168, s32[512]{0:T(512)S(1)} %get-tuple-element.169, s32[2048]{0:T(1024)S(1)} %broadcast_multiply_fusion.4, pred[]{:T(512)S(6)} %compare.3, f32[4096,256]{1,0:T(8,128)} %get-tuple-element.188, ...), kind=kOutput, calls=%fused_computation.36.clone.1 | convolution fusion | flops 3257925632 | bytes 4730885 | tf_op jit(solution)/shard_map/while/body/eval_jaxpr/dot_general | solution.py:41
  154.8 24.2 %fusion.75 = f32[256,2048]{1,0:T(8,128)S(1)} fusion(f32[256,2048]{1,0:T(8,128)S(1)} %get-tuple-element.179, s32[512]{0:T(512)S(1)} %get-tuple-element.168, s32[512]{0:T(512)S(1)} %get-tuple-element.169, s32[2048]{0:T(1024)S(1)} %broadcast_multiply_fusion.4, pred[]{:T(512)S(6)} %compare.3, f32[4096,256]{1,0:T(8,128)} %get-tuple-element.188, ...), kind=kOutput, calls=%fused_computation.36.clone.1 | convolution fusion | flops 3257925632 | bytes 4730885 | tf_op jit(solution)/shard_map/while/body/eval_jaxpr/dot_general | solution.py:41
  179.1 24.2 %fusion.75 = f32[256,2048]{1,0:T(8,128)S(1)} fusion(f32[256,2048]{1,0:T(8,128)S(1)} %get-tuple-element.179, s32[512]{0:T(512)S(1)} %get-tuple-element.168, s32[512]{0:T(512)S(1)} %get-tuple-element.169, s32[2048]{0:T(1024)S(1)} %broadcast_multiply_fusion.4, pred[]{:T(512)S(6)} %compare.3, f32[4096,256]{1,0:T(8,128)} %get-tuple-element.188, ...), kind=kOutput, calls=%fused_computation.36.clone.1 | convolution fusion | flops 3257925632 | bytes 4730885 | tf_op jit(solution)/shard_map/while/body/eval_jaxpr/dot_general | solution.py:41
  203.4 24.2 %fusion.75 = f32[256,2048]{1,0:T(8,128)S(1)} fusion(f32[256,2048]{1,0:T(8,128)S(1)} %get-tuple-element.179, s32[512]{0:T(512)S(1)} %get-tuple-element.168, s32[512]{0:T(512)S(1)} %get-tuple-element.169, s32[2048]{0:T(1024)S(1)} %broadcast_multiply_fusion.4, pred[]{:T(512)S(6)} %compare.3, f32[4096,256]{1,0:T(8,128)} %get-tuple-element.188, ...), kind=kOutput, calls=%fused_computation.36.clone.1 | convolution fusion | flops 3257925632 | bytes 4730885 | tf_op jit(solution)/shard_map/while/body/eval_jaxpr/dot_general | solution.py:41
  227.6 24.2 %fusion.75 = f32[256,2048]{1,0:T(8,128)S(1)} fusion(f32[256,2048]{1,0:T(8,128)S(1)} %get-tuple-element.179, s32[512]{0:T(512)S(1)} %get-tuple-element.168, s32[512]{0:T(512)S(1)} %get-tuple-element.169, s32[2048]{0:T(1024)S(1)} %broadcast_multiply_fusion.4, pred[]{:T(512)S(6)} %compare.3, f32[4096,256]{1,0:T(8,128)} %get-tuple-element.188, ...), kind=kOutput, calls=%fused_computation.36.clone.1 | convolution fusion | flops 3257925632 | bytes 4730885 | tf_op jit(solution)/shard_map/while/body/eval_jaxpr/dot_general | solution.py:41
  251.9 24.2 %fusion.75 = f32[256,2048]{1,0:T(8,128)S(1)} fusion(f32[256,2048]{1,0:T(8,128)S(1)} %get-tuple-element.179, s32[512]{0:T(512)S(1)} %get-tuple-element.168, s32[512]{0:T(512)S(1)} %get-tuple-element.169, s32[2048]{0:T(1024)S(1)} %broadcast_multiply_fusion.4, pred[]{:T(512)S(6)} %compare.3, f32[4096,256]{1,0:T(8,128)} %get-tuple-element.188, ...), kind=kOutput, calls=%fused_computation.36.clone.1 | convolution fusion | flops 3257925632 | bytes 4730885 | tf_op jit(solution)/shard_map/while/body/eval_jaxpr/dot_general | solution.py:41
  276.2 24.2 %fusion.75 = f32[256,2048]{1,0:T(8,128)S(1)} fusion(f32[256,2048]{1,0:T(8,128)S(1)} %get-tuple-element.179, s32[512]{0:T(512)S(1)} %get-tuple-element.168, s32[512]{0:T(512)S(1)} %get-tuple-element.169, s32[2048]{0:T(1024)S(1)} %broadcast_multiply_fusion.4, pred[]{:T(512)S(6)} %compare.3, f32[4096,256]{1,0:T(8,128)} %get-tuple-element.188, ...), kind=kOutput, calls=%fused_computation.36.clone.1 | convolution fusion | flops 3257925632 | bytes 4730885 | tf_op jit(solution)/shard_map/while/body/eval_jaxpr/dot_general | solution.py:41
  300.4 0.0 copy-done.1
  300.4 1.7 fusion.69
  302.1 32.0 %psum.7 = f32[2048]{0:T(1024)S(1)} all-reduce(f32[2048]{0:T(1024)S(1)} %get-tuple-element.137), channel_id=1, replica_groups=mesh['grp'=2,'mode'=8,'node'=2] {'mode','node'}, use_global_device_ids=true, to_apply=%region_3.0 | all-reduce | flops 2048 | bytes 16384 | tf_op jit(solution)/shard_map/psum | solution.py:58
  334.1 0.6 broadcast_multiply_fusion.2
  (17 shorter events, 0.1 us)
Async XLA Ops:
  5.5 100.7 %copy-start = (s32[2048]{0:T(1024)S(1)}, s32[2048]{0:T(1024)}, u32[]{:S(2)}) copy-start(s32[2048]{0:T(1024)} %param.9) | copy-start | bytes 24580
  5.5 100.7 %all-to-all-start = ((f32[512,8,256]{2,0,1:T(8,128)}), f32[512,8,256]{2,0,1:T(8,128)}, u32[]{:S(2)}, u32[]{:S(2)}) async-start(f32[512,8,256]{2,0,1:T(8,128)} %bitcast.8), calls=%async_computation | async-start | bytes 8388608 | tf_op jit(solution)/shard_map/all_to_all | solution.py:55
  106.2 194.2 %copy-start.1 = (f32[256]{0:T(256)S(1)}, f32[256]{0:T(256)}, u32[]{:S(2)}) copy-start(f32[256]{0:T(256)} %param.8) | copy-start | bytes 3076
where the time goes:
time: 335 us
  matrix products  194 us (58%)
  waiting for transfers between devices  93.3 us (28%)
  blocking collectives  32 us (10%)
  starting transfers between devices  7.41 us (2%)
  other arithmetic  4.88 us (1%)
    dot_general x8, matrix products, add_block(): lax.dot_general(rows, coeffs, (((0,), (0,)), ((), ())), precision=lax.Pre...  194 us
    all_to_all x1, waiting for transfers between devices, on_device(): lax.all_to_all(scaled, 'mode', split_axis=1, concat_axis=0, tiled=True)  93.3 us
    psum x1, blocking collectives, on_device(): totals = lax.psum(jnp.sum(modulus, axis=0), ('mode', 'node'))  32 us
    all_to_all x1, starting transfers between devices, on_device(): lax.all_to_all(scaled, 'mode', split_axis=1, concat_axis=0, tiled=True)  7.41 us
  transfers between devices with their start and end apart: 1, of which 1 were waited for; matrix products, arithmetic and copies ran while one was open for 0% of the time, Pallas kernels for 0%

commit v1 on v0

v1 whole, which is shorter than its diff:
```python
import functools

import jax
import jax.numpy as jnp
from jax import lax
from jax.experimental import pallas as pl
from jax.experimental.pallas import tpu as pltpu
from jax.sharding import PartitionSpec as P

SEED_FACTOR = -1640531527
COUNT_FACTOR = 668265261
COS_TERMS = (1.4142134962552295, -6.97885094856384, 5.73946037690727, -1.8835579059862844, 0.31068802752475627)
SUB = 16


def scramble(word):
    word = word ^ lax.shift_right_logical(word, 15)
    word = word * -2048144789
    word = word ^ lax.shift_right_logical(word, 13)
    word = word * -1028477387
    return word ^ lax.shift_right_logical(word, 16)


def normals(first):
    one = scramble(first) & 16777215
    two = scramble(first + COUNT_FACTOR) << 8
    first_unit = one.astype(jnp.float32) * (1.0 / 16777216.0) + (0.5 / 16777216.0)
    turn = two.astype(jnp.float32) * (2.0**-32) + (0.5 / 16777216.0)
    square = jnp.maximum(-2.0 * jnp.log(first_unit), 1e-30)
    radius = square * lax.rsqrt(square)
    arg = turn * turn
    half = jnp.float32(COS_TERMS[-1])
    for term in COS_TERMS[-2::-1]:
        half = half * arg + jnp.float32(term)
    return radius * (half * half - 1.0)


def split(values):
    high = values.astype(jnp.bfloat16)
    return high, (values - high.astype(jnp.float32)).astype(jnp.bfloat16)


def fill_rows(seeds_ref, high_ref, low_ref, first_mode, rows):
    samples = seeds_ref.shape[1]
    row_terms = lax.broadcasted_iota(jnp.int32, (SUB, 128), 0) * (2 * COUNT_FACTOR % 2**32 - (2**32 if 2 * COUNT_FACTOR % 2**32 >= 2**31 else 0))

    def group(i, carry):
        start = pl.multiple_of(i * SUB, SUB)
        mode_terms = row_terms + (first_mode + start) * 2 * COUNT_FACTOR
        for at in range(0, samples, 128):
            first = seeds_ref[:, at:at + 128] * SEED_FACTOR + mode_terms
            high, low = split(normals(first))
            high_ref[pl.ds(start, SUB), at:at + 128] = high
            low_ref[pl.ds(start, SUB), at:at + 128] = low
        return carry

    lax.fori_loop(0, rows // SUB, group, 0)


def draw_kernel(rows, seeds_ref, high_ref, low_ref):
    fill_rows(seeds_ref, high_ref, low_ref, pl.program_id(0) * rows, rows)


def draw(seeds, modes):
    rows = 256
    samples = seeds.shape[1]
    out = jax.ShapeDtypeStruct((modes, samples), jnp.bfloat16)
    spec = pl.BlockSpec((rows, samples), lambda i: (i, 0))
    return pl.pallas_call(
        functools.partial(draw_kernel, rows),
        grid=(modes // rows,),
        in_specs=[pl.BlockSpec((1, samples), lambda i: (0, 0))],
        out_specs=[spec, spec],
        out_shape=[out, out],
        name="draw",
    )(seeds)


def dot(a, b):
    return lax.dot_general(a, b, (((0,), (0,)), ((), ())), preferred_element_type=jnp.float32)


def contract_kernel(basis_ref, high_ref, low_ref, mean_ref, out_ref, sum_ref):
    step = pl.program_id(0)

    @pl.when(step == 0)
    def _():
        out_ref[...] = jnp.zeros_like(out_ref)

    basis_high, basis_low = split(basis_ref[...])
    out_ref[...] += dot(basis_high, high_ref[...]) + dot(basis_high, low_ref[...]) + dot(basis_low, high_ref[...])

    @pl.when(step == pl.num_programs(0) - 1)
    def _():
        modulus = jnp.exp(out_ref[...] + mean_ref[...])
        out_ref[...] = modulus
        sum_ref[...] = jnp.sum(modulus, axis=0, keepdims=True)


def contract(basis, high, low, mean):
    rows = 512
    modes, nodes = basis.shape
    samples = high.shape[1]
    spec = pl.BlockSpec((rows, samples), lambda i: (i, 0))
    return pl.pallas_call(
        contract_kernel,
        grid=(modes // rows,),
        in_specs=[pl.BlockSpec((rows, nodes), lambda i: (i, 0)), spec, spec, pl.BlockSpec((nodes, 1), lambda i: (0, 0))],
        out_specs=[pl.BlockSpec((nodes, samples), lambda i: (0, 0)), pl.BlockSpec((1, samples), lambda i: (0, 0))],
        out_shape=[jax.ShapeDtypeStruct((nodes, samples), jnp.float32), jax.ShapeDtypeStruct((1, samples), jnp.float32)],
        name="contract",
    )(basis, high, low, mean)


def on_device(mode_basis, mode_scales, mean_log, sample_seeds):
    own_rows = mean_log.shape[0]
    scaled = mode_scales[:, None] * mode_basis
    gathered = lax.all_to_all(scaled, "mode", split_axis=1, concat_axis=0, tiled=True)
    high, low = draw(sample_seeds[None, :], gathered.shape[0])
    modulus, sums = contract(gathered, high, low, mean_log[:, None])
    totals = lax.psum(sums[0], ("mode", "node"))
    node_count = own_rows * lax.axis_size("mode") * lax.axis_size("node")
    return (modulus, totals / node_count)


def solution(mesh):
    return jax.shard_map(
        on_device,
        mesh=mesh,
        in_specs=(P("mode", "node"), P("mode"), P(("node", "mode")), P("grp")),
        out_specs=(P(("node", "mode"), "grp"), P("grp")),
        check_vma=False,
    )
```

time: 335 us -> 161 us (0.48)
  matrix products: 194 us -> 0 us
  Pallas kernels: 0 us -> 82.3 us
  waiting for transfers between devices: 93.3 us -> 31.5 us
    dot_general x8 -> x0, matrix products: 194 us -> none  [add_block(): lax.dot_general(rows, coeffs, (((0,), (0,)), ((), ())), precision=lax.Pre...]
    pallas_call x0 -> x2, Pallas kernels: none -> 82.3 us  [the longest x1 60.9 us: draw(): pl.pallas_call(functools.partial(draw_kernel, rows), grid=(modes // rows,...]
    all_to_all x1, waiting for transfers between devices: 93.3 us -> 31.5 us  [on_device(): lax.all_to_all(scaled, 'mode', split_axis=1, concat_axis=0, tiled=True)]
  transfers between devices with their start and end apart: 1 -> 1, of which waited for: 1 -> 1; matrix products, arithmetic and copies ran while one was open for 0% -> 0% of each run, Pallas kernels for 0% -> 38%
where the time goes in v1:
time: 161 us; the launch traced here: 160 us
  Pallas kernels  82.3 us (51%)
  blocking collectives  32.1 us (20%)
  waiting for transfers between devices  31.5 us (20%)
  starting transfers between devices  7.41 us (5%)
  local copies, waits for them, and re-layouts  3.15 us (2%)
  other arithmetic  3.13 us (2%)
    pallas_call x1, Pallas kernels, draw(): pl.pallas_call(functools.partial(draw_kernel, rows), grid=(modes // rows,...  60.9 us
    psum x1, blocking collectives, on_device(): totals = lax.psum(sums[0], ('mode', 'node'))  32.1 us
    all_to_all x1, waiting for transfers between devices, on_device(): lax.all_to_all(scaled, 'mode', split_axis=1, concat_axis=0, tiled=True)  31.5 us
    pallas_call x1, Pallas kernels, contract(): pl.pallas_call(contract_kernel, grid=(modes // rows,), in_specs=[pl.Block...  21.3 us
    all_to_all x1, starting transfers between devices, on_device(): lax.all_to_all(scaled, 'mode', split_axis=1, concat_axis=0, tiled=True)  7.41 us
  transfers between devices with their start and end apart: 1, of which 1 were waited for; matrix products, arithmetic and copies ran while one was open for 0% of the time, Pallas kernels for 38%

profile of v1, /device:TPU:0, one launch (start us, length us, event | category | flops | bytes accessed | tf_op | source)
XLA Modules:
  0.0 160.3 jit_solution(8849742231954847420)
XLA Ops:
  0.6 2.5 %broadcast_multiply_fusion = f32[512,2048]{1,0:T(8,128)S(1)} fusion(f32[512,2048]{1,0:T(8,128)} %param.4, f32[512]{0:T(512)} %param.5), kind=kLoop, calls=%fused_computation.1 | loop fusion | flops 1048576 | bytes 8390656 | tf_op jit(solution)/shard_map/mul | solution.py:117
  3.2 2.4 %copy.11 = f32[64,8,8,256]{3,2,0,1:T(8,128)} copy(f32[64,8,8,256]{3,2,1,0:T(8,128)S(1)} %bitcast.10) | data formatting | bytes 8388608 | tf_op jit(solution)/shard_map/all_to_all | solution.py:118
  5.5 0.0 copy-start
  5.5 7.4 %all-to-all-start = ((f32[512,8,256]{2,0,1:T(8,128)}), f32[512,8,256]{2,0,1:T(8,128)}, u32[]{:S(2)}, u32[]{:S(2)}) async-start(f32[512,8,256]{2,0,1:T(8,128)} %bitcast.11), calls=%async_computation | async-start | bytes 8388608 | tf_op jit(solution)/shard_map/all_to_all | solution.py:118
  12.9 0.0 copy-done
  12.9 0.8 copy.8.mean_ref
  13.7 60.9 %draw.1 = (bf16[4096,2048]{1,0:T(8,128)(2,1)}, bf16[4096,2048]{1,0:T(8,128)(2,1)}) custom-call(s32[1,2048]{1,0:T(1,128)} %bitcast.12), custom_call_target="tpu_custom_call" | custom-call | tf_op jit(solution)/shard_map/draw/pallas_call | solution.py:69
  74.7 31.5 %all-to-all-done = f32[512,8,256]{2,0,1:T(8,128)} async-done(((f32[512,8,256]{2,0,1:T(8,128)}), f32[512,8,256]{2,0,1:T(8,128)}, u32[]{:S(2)}, u32[]{:S(2)}) %all-to-all-start) | async-done | bytes 4194336 | tf_op jit(solution)/shard_map/all_to_all | solution.py:118
  106.2 21.3 %contract.1 = (f32[256,2048]{1,0:T(8,128)}, f32[1,2048]{1,0:T(1,128)}) custom-call(f32[4096,256]{1,0:T(8,128)} %bitcast.1.basis_ref, bf16[4096,2048]{1,0:T(8,128)(2,1)} %get-tuple-element.6.high_ref, bf16[4096,2048]{1,0:T(8,128)(2,1)} %get-tuple-element.7.low_ref, f32[256,1]{1,0:T(8,128)} %copy.8.mean_ref), custom_call_target="tpu_custom_call" | custom-call | tf_op jit(solution)/shard_map/contract/pallas_call | solution.py:105
  127.6 32.1 %psum.7 = f32[2048]{0:T(1024)S(1)} all-reduce(f32[2048]{0:T(1024)} %bitcast.13), channel_id=1, replica_groups=mesh['grp'=2,'mode'=8,'node'=2] {'mode','node'}, use_global_device_ids=true, to_apply=%region_0.0 | all-reduce | flops 2048 | bytes 16384 | tf_op jit(solution)/shard_map/psum | solution.py:121
  159.7 0.6 broadcast_multiply_fusion.1
Async XLA Ops:
  5.5 7.4 %copy-start = (f32[256]{0:T(256)S(1)}, f32[256]{0:T(256)}, u32[]{:S(2)}) copy-start(f32[256]{0:T(256)} %param.6) | copy-start | bytes 3076
  5.5 100.7 %all-to-all-start = ((f32[512,8,256]{2,0,1:T(8,128)}), f32[512,8,256]{2,0,1:T(8,128)}, u32[]{:S(2)}, u32[]{:S(2)}) async-start(f32[512,8,256]{2,0,1:T(8,128)} %bitcast.11), calls=%async_computation | async-start | bytes 8388608 | tf_op jit(solution)/shard_map/all_to_all | solution.py:118
